TPU v7x, 32 devices: a whole 2x2x4 slice. The times are simulated.
32 devices in a mesh: grp: 2 (over x), src: 8 (over z, y), tgt: 2 (over core).
Axes of the slice: x: 2, y: 2, z: 4, core: 2. Of those that a mesh axis runs over, the one named last changes fastest.
Arguments:
- densities: bfloat16 [512, 32768], P('grp', ('src', 'tgt')), parts along dimension 0, may hold values from -6 to 6
- compress: bfloat16 [65536, 2, 256], P(('grp', 'src', 'tgt')), parts along dimension 0, may hold values from -0.0625 to 0.0625
- level_a: bfloat16 [6, 2048, 2, 256], P('grp', 'src', None, 'tgt'), parts along dimension 0, may hold values from -0.1875 to 0.1875
- level_b: bfloat16 [6, 2048, 2, 256], P('grp', 'src', None, 'tgt'), parts along dimension 0, may hold values from -0.1875 to 0.1875
- expand: bfloat16 [4096, 2, 4096], P(('grp', 'src'), None, 'tgt'), parts along dimension 0, may hold values from -0.25 to 0.25
- near_tiles: bfloat16 [2048, 128, 2, 128], P(('grp', 'src', 'tgt')), parts along dimension 0, may hold values from -0.375 to 0.375
- tile_pairs: int32 [2048, 2], P(('grp', 'src', 'tgt')), parts along dimension 0, may hold values from 0 to 15
- tile_count: int32 [32], P(('grp', 'src', 'tgt')), parts along dimension 0, may hold values from 1 to 63, as said below
- cluster_order: int32 [32, 16], P(('grp', 'src', 'tgt')), parts along dimension 0, may hold values from 0 to 15, each once within a row
Outputs:
- potential: bfloat16 [512, 32768], P('grp', ('src', 'tgt')), parts along dimension 0
There are 2 independent parts, one for each index of `grp`. A program takes and returns all parts, laid end to end along the dimension named above; each array names one. Nothing has to cross between parts.
Inputs may be any that keep to these rules, and one draw needn't show every extreme that they name: For every i below 8, tile_count[i] + tile_count[i + 8] == 64; slots at or beyond a device's count are unused. `cluster_order`: each row is a permutation.
All inputs are finite; a program needn't handle non-finite values.
Results may differ from a plain program's by a relative error of at most 0.007.
Values may be sent and summed in bfloat16 or wider, within the bound.
A program may use at most 128 MiB of HBM per device.

v0:
```python
import functools

import jax
import jax.numpy as jnp
from jax import lax
from jax.experimental import pallas as pl
from jax.experimental.pallas import tpu as pltpu
from jax.sharding import PartitionSpec as P

MESH = pl.DeviceIdType.MESH
CHUNKS = 2
UNROLL = 4


def lift(real, imag, perm):
    upper = jnp.concatenate([real, -imag], axis=1)
    lower = jnp.concatenate([imag, real], axis=1)
    both = jnp.concatenate([upper, lower], axis=0)
    return jnp.dot(both, perm, preferred_element_type=jnp.float32).astype(jnp.bfloat16)


def flat(block):
    return block.reshape(block.shape[0] * 2, block.shape[2])


def kernel(
    sizes,
    dens_h, comp_h, la_h, lb_h, exp_h, tiles_h, pairs_s, count_s, order_s,
    out_h,
    dens_v, comp_v, lev_v, exp_v, tiles_v, lifted_v, sums_v, part_v, part_r, coef_v, recv_v, fin_v, out_v,
    dens_sem, comp_sem, lev_sem, levs_sem, levr_sem, exp_sem, tiles_sem, part_sem, send_sem, recv_sem, fin_sem, out_sem,
):
    levels, clusters, width, slots, rhs, rank, n_tgt = sizes
    src, tgt = lax.axis_index("src"), lax.axis_index("tgt")
    other = 1 - tgt
    sibling = {"tgt": other}
    partners = [{"src": src ^ (1 << level)} for level in range(levels)]
    lanes = rank // width
    comp_parts = comp_sem.shape[1]
    rows_part = comp_h.shape[0] // comp_parts
    tile_parts = tiles_sem.shape[0]
    slots_part = slots // tile_parts

    loads_dens = pltpu.make_async_copy(dens_h, dens_v, dens_sem)
    loads_dens.start()
    loads_comp = [
        [
            pltpu.make_async_copy(
                comp_h.at[pl.ds(part * rows_part, rows_part), :, pl.ds(lane * width, width)],
                comp_v.at[lane, pl.ds(part * rows_part, rows_part)],
                comp_sem.at[lane, part],
            )
            for lane in range(lanes)
        ]
        for part in range(comp_parts)
    ]
    for part in loads_comp:
        for item in part:
            item.start()
    barrier = pltpu.get_barrier_semaphore()
    for target in [sibling] + partners:
        pl.semaphore_signal(barrier, inc=1, device_id=target, device_id_type=MESH)
    factors = (la_h, lb_h)
    loads_lev = [pltpu.make_async_copy(factors[ab], lev_v.at[ab, tgt], lev_sem.at[ab]) for ab in range(2)]
    for item in loads_lev:
        item.start()
    loads_tiles = [
        pltpu.make_async_copy(
            tiles_h.at[pl.ds(part * slots_part, slots_part)],
            tiles_v.at[pl.ds(part * slots_part, slots_part)],
            tiles_sem.at[part],
        )
        for part in range(tile_parts)
    ]
    for item in loads_tiles:
        item.start()
    loads_exp = [
        pltpu.make_async_copy(exp_h.at[:, :, pl.ds(c * width, width)], exp_v.at[c], exp_sem.at[c])
        for c in range(clusters)
    ]
    for item in loads_exp:
        item.start()

    row = lax.broadcasted_iota(jnp.int32, (2 * width, 2 * width), 0)
    col = lax.broadcasted_iota(jnp.int32, (2 * width, 2 * width), 1)
    spot = jnp.where(row < width, 2 * row, 2 * (row - width) + 1)
    perm = (spot == col).astype(jnp.float32).astype(jnp.bfloat16)

    pl.semaphore_wait(barrier, 1 + levels)
    swaps_lev = [
        pltpu.make_async_remote_copy(
            src_ref=factors[ab], dst_ref=lev_v.at[ab, tgt], send_sem=levs_sem.at[ab], recv_sem=levr_sem.at[ab],
            device_id=sibling, device_id_type=MESH,
        )
        for ab in range(2)
    ]
    for item in swaps_lev:
        item.start()

    loads_dens.wait()
    for c in range(clusters):
        cut = pl.ds(c * width, width)
        lifted_v[c] = lift(dens_v[:rhs, cut], dens_v[rhs:, cut], perm)
    per_part = clusters // comp_parts
    sums = [jnp.zeros((2 * rhs, width), jnp.float32) for _ in range(lanes)]
    for part in range(comp_parts):
        for item in loads_comp[part]:
            item.wait()
        for c in range(part * per_part, (part + 1) * per_part):
            block = lifted_v[c]
            for lane in range(lanes):
                sums[lane] = sums[lane] + jnp.dot(
                    block, flat(comp_v[lane, pl.ds(c * width, width)]), preferred_element_type=jnp.float32
                )
    half = rhs // n_tgt
    for h in range(n_tgt):
        for ri in range(2):
            for lane in range(lanes):
                part_v[h, ri, :, pl.ds(lane * width, width)] = sums[lane][ri * rhs + h * half : ri * rhs + (h + 1) * half]
    swap_part = pltpu.make_async_remote_copy(
        src_ref=part_v.at[other], dst_ref=part_r, send_sem=part_sem.at[0], recv_sem=part_sem.at[1],
        device_id=sibling, device_id_type=MESH,
    )
    swap_part.start()

    rows = half // CHUNKS

    def send(level, q):
        copy = pltpu.make_async_remote_copy(
            src_ref=coef_v.at[level, q], dst_ref=recv_v.at[level, q],
            send_sem=send_sem.at[level, q], recv_sem=recv_sem.at[level, q],
            device_id=partners[level], device_id_type=MESH,
        )
        copy.start()
        return copy

    def lifted(value):
        return jnp.concatenate(
            [
                lift(value[0, :, lane * width : (lane + 1) * width], value[1, :, lane * width : (lane + 1) * width], perm)
                for lane in range(lanes)
            ],
            axis=1,
        )

    def apply(value, ab, level):
        return jnp.concatenate(
            [
                jnp.dot(value, flat(lev_v[ab, h, level]), preferred_element_type=jnp.float32)
                for h in range(n_tgt)
            ],
            axis=1,
        )

    count = count_s[0]
    last = [jnp.int32(slots) for _ in range(clusters)]
    sums_v[slots] = jnp.zeros((2 * rhs, width), jnp.float32)

    def near_step(step, last):
        last = list(last)
        base = step * UNROLL
        terms = [
            jnp.dot(lifted_v[pairs_s[1, base + u]], flat(tiles_v[base + u]), preferred_element_type=jnp.float32)
            for u in range(UNROLL)
        ]
        for u in range(UNROLL):
            slot = base + u
            target = pairs_s[0, slot]
            active = slot < count
            before = jnp.int32(slots)
            for c in range(clusters):
                hit = target == c
                before = jnp.where(hit, last[c], before)
                last[c] = jnp.where(hit & active, slot, last[c])
            sums_v[slot] = terms[u] + sums_v[before]
        return tuple(last)

    swap_part.wait()
    sends = []
    for q in range(CHUNKS):
        cut = pl.ds(q * rows, rows)
        coef_v[0, q] = (part_v[tgt, :, cut, :] + part_r[:, cut, :]).astype(jnp.bfloat16)
        sends.append(send(0, q))
    for item in loads_lev:
        item.wait()
    for item in swaps_lev:
        item.wait()
    current = sends
    done_sends = []
    swaps_fin = []
    tiles_waited = 0
    for level in range(levels):
        own = [apply(lifted(coef_v[level, q]), 0, level) for q in range(CHUNKS)]
        first, final = (tile_parts * level) // levels, (tile_parts * (level + 1)) // levels
        for part in range(first, final):
            loads_tiles[part].wait()
        last = lax.fori_loop(
            first * slots_part // UNROLL, final * slots_part // UNROLL, near_step, tuple(last)
        )
        following = []
        for q in range(CHUNKS):
            current[q].wait_recv()
            total = own[q] + apply(lifted(recv_v[level, q]), 1, level)
            fresh = jnp.stack([total[:rows], total[rows:]]).astype(jnp.bfloat16)
            if level + 1 < levels:
                coef_v[level + 1, q] = fresh
                following.append(send(level + 1, q))
            else:
                fin_v[tgt, q] = fresh
                copy = pltpu.make_async_remote_copy(
                    src_ref=fin_v.at[tgt, q], dst_ref=fin_v.at[tgt, q],
                    send_sem=fin_sem.at[0, q], recv_sem=fin_sem.at[1, q],
                    device_id=sibling, device_id_type=MESH,
                )
                copy.start()
                swaps_fin.append(copy)
        done_sends += current
        current = following
    for item in loads_exp:
        item.wait()
    for item in swaps_fin:
        item.wait()
    for item in done_sends:
        item.wait_send()

    whole = [
        jnp.concatenate([fin_v[h, q, ri] for h in range(n_tgt) for q in range(CHUNKS)], axis=0) for ri in range(2)
    ]
    operand = jnp.concatenate(
        [
            lift(whole[0][:, lane * width : (lane + 1) * width], whole[1][:, lane * width : (lane + 1) * width], perm)
            for lane in range(lanes)
        ],
        axis=1,
    )
    out_parts = out_sem.shape[0]
    per_out = clusters // out_parts
    stores = []
    for part in range(out_parts):
        for t in range(part * per_out, (part + 1) * per_out):
            origin = jnp.int32(0)
            for c in range(clusters):
                origin = jnp.where(order_s[0, c] == t, c, origin)
            far = jnp.dot(operand, flat(exp_v[origin]), preferred_element_type=jnp.float32)
            out_v[:, pl.ds(t * width, width)] = (far + sums_v[last[t]]).astype(jnp.bfloat16)
        cut = pl.ds(part * per_out * width, per_out * width)
        stores.append(pltpu.make_async_copy(out_v.at[:, cut], out_h.at[:, cut], out_sem.at[part]))
        stores[-1].start()
    for item in stores:
        item.wait()


def shards(
    densities, compress, level_a, level_b, expand, near_tiles, tile_pairs, tile_count, cluster_order
):
    row_count, points = densities.shape
    rhs = row_count // 2
    rank = compress.shape[2]
    levels = level_a.shape[0]
    clusters = cluster_order.shape[1]
    width = points // clusters
    slots = near_tiles.shape[0]
    n_tgt = lax.axis_size("tgt")
    sizes = (levels, clusters, width, slots, rhs, rank, n_tgt)
    lanes = rank // width
    rows = rhs // n_tgt // CHUNKS
    comp_parts, tile_parts, out_parts = 4, 16, 4
    bf16, f32 = jnp.bfloat16, jnp.float32
    anywhere = pl.BlockSpec(memory_space=pl.ANY)
    scalar = pl.BlockSpec(memory_space=pltpu.SMEM)
    dma = pltpu.SemaphoreType.DMA
    return pl.pallas_call(
        functools.partial(kernel, sizes),
        out_shape=jax.ShapeDtypeStruct((row_count, points), bf16),
        in_specs=[anywhere] * 6 + [scalar] * 3,
        out_specs=anywhere,
        scratch_shapes=[
            pltpu.VMEM((row_count, points), bf16),
            pltpu.VMEM((lanes, points, 2, width), bf16),
            pltpu.VMEM((2, n_tgt, levels, rank, 2, width), bf16),
            pltpu.VMEM((clusters, rank, 2, width), bf16),
            pltpu.VMEM((slots, width, 2, width), bf16),
            pltpu.VMEM((clusters, row_count, 2 * width), bf16),
            pltpu.VMEM((slots + 1, row_count, width), f32),
            pltpu.VMEM((n_tgt, 2, rhs // n_tgt, rank), f32),
            pltpu.VMEM((2, rhs // n_tgt, rank), f32),
            pltpu.VMEM((levels, CHUNKS, 2, rows, rank), bf16),
            pltpu.VMEM((levels, CHUNKS, 2, rows, rank), bf16),
            pltpu.VMEM((n_tgt, CHUNKS, 2, rows, rank), bf16),
            pltpu.VMEM((row_count, points), bf16),
            dma,
            dma((lanes, comp_parts)),
            dma((2,)),
            dma((2,)),
            dma((2,)),
            dma((clusters,)),
            dma((tile_parts,)),
            dma((2,)),
            dma((levels, CHUNKS)),
            dma((levels, CHUNKS)),
            dma((2, CHUNKS)),
            dma((out_parts,)),
        ],
        compiler_params=pltpu.CompilerParams(collective_id=0, has_side_effects=True),
    )(densities, compress, level_a, level_b, expand, near_tiles, tile_pairs.T, tile_count, cluster_order)


def solution(mesh):
    placed = (
        P("grp", ("src", "tgt")),
        P(("grp", "src", "tgt"), None, None),
        P("grp", "src", None, "tgt"),
        P("grp", "src", None, "tgt"),
        P(("grp", "src"), None, "tgt"),
        P(("grp", "src", "tgt"), None, None, None),
        P(("grp", "src", "tgt"), None),
        P(("grp", "src", "tgt")),
        P(("grp", "src", "tgt"), None),
    )
    return jax.shard_map(
        shards, mesh=mesh, in_specs=placed, out_specs=P("grp", ("src", "tgt")), check_vma=False
    )
```

profile of v0, /device:TPU:0, one launch (start us, length us, event | category | flops | bytes accessed | tf_op | source)
XLA Modules:
  0.0 28.0 jit_solution(8164705942211654304)
XLA Ops:
  0.7 25.0 %shard_map.91 = bf16[256,2048]{1,0:T(8,128)(2,1)} custom-call(bf16[256,2048]{1,0:T(8,128)(2,1)} %dens_h.1, bf16[2048,2,256]{2,1,0:T(2,128)(2,1)} %comp_h.1, bf16[3,256,2,128]{3,2,1,0:T(2,128)(2,1)} %la_h.1, bf16[3,256,2,128]{3,2,1,0:T(2,128)(2,1)} %lb_h.1, bf16[256,2,2048]{2,1,0:T(2,128)(2,1)} %exp_h.1, bf16[64,128,2,128]{3,2,1,0:T(2,128)(2,1)} %tiles_h.1, ...), custom_call_target="tpu_custom_call" | custom-call | tf_op jit(solution)/shard_map/pallas_call | solution.py:272
  25.7 2.3 %copy.12 = bf16[256,2048]{1,0:T(8,128)(2,1)} copy(bf16[256,2048]{1,0:T(8,128)(2,1)} %shard_map.91) | data formatting | bytes 2097152
where the time goes:
time: 28.1 us; the launch traced here: 28 us
  Pallas kernels  25 us (89%)
  local copies, waits for them, and re-layouts  2.3 us (8%)
  between operations  0.66 us (2%)
    pallas_call x1, Pallas kernels, shards(): pl.pallas_call(functools.partial(kernel, sizes), out_shape=jax.ShapeDtype...  25 us
    unnamed x1, local copies, waits for them, and re-layouts  2.3 us

commit v1 on v0

v1 whole, which is shorter than its diff:
```python
import functools

import jax
import jax.numpy as jnp
from jax import lax
from jax.experimental import pallas as pl
from jax.experimental.pallas import tpu as pltpu
from jax.sharding import PartitionSpec as P

MESH = pl.DeviceIdType.MESH
CHUNKS = 2
UNROLL = 4
BF16, F32 = jnp.bfloat16, jnp.float32


def matmul(a, b):
    return jnp.dot(a, b, preferred_element_type=F32)


def spread(width, grouped):
    row = lax.broadcasted_iota(jnp.int32, (2 * width, 2 * width), 0)
    col = lax.broadcasted_iota(jnp.int32, (2 * width, 2 * width), 1)
    imag = row >= width
    point = jnp.where(imag, row - width, row)
    if grouped:
        within = point & 7
        point = (point - within) + jnp.where(within < 4, 2 * within, 2 * within - 7)
    one, zero = jnp.ones(row.shape, F32), jnp.zeros(row.shape, F32)
    signed = jnp.where(imag, -one, one)
    upper = jnp.where(jnp.where(imag, 2 * point + 1, 2 * point) == col, signed, zero)
    lower = jnp.where(jnp.where(imag, 2 * point, 2 * point + 1) == col, one, zero)
    return upper.astype(BF16), lower.astype(BF16)


def kernel(
    sizes,
    dens_h, comp_h, la_h, lb_h, exp_h, tiles_h, pairs_h, order_h, count_s,
    out_v,
    dens_v, comp_v, compd_v, lev_v, big_v, expt_v, exp_v, tiles_v, liftc_v, lifted_v, sums_v,
    part_v, part_r, coef_v, recv_v, fin_r, pairs_s, order_s,
    dens_sem, comp_sem, lev_sem, levs_sem, levr_sem, exp_sem, expt_sem, tiles_sem, part_sem, send_sem, recv_sem,
    fin_sem, table_sem,
):
    levels, clusters, width, slots, rhs, rank, n_tgt = sizes
    src, tgt = lax.axis_index("src"), lax.axis_index("tgt")
    other = 1 - tgt
    sibling = {"tgt": other}
    partners = [{"src": src ^ (1 << level)} for level in range(levels)]
    lanes = rank // width
    comp_parts = comp_sem.shape[0]
    comp_rows = comp_h.shape[0] // comp_parts
    tile_parts = tiles_sem.shape[0]
    slots_part = slots // tile_parts
    half = rhs // n_tgt
    rows = half // CHUNKS

    loads_dens = pltpu.make_async_copy(dens_h, dens_v, dens_sem)
    loads_dens.start()
    loads_comp = [
        pltpu.make_async_copy(
            comp_h.at[pl.ds(part * comp_rows, comp_rows)], comp_v.at[pl.ds(part * comp_rows, comp_rows)],
            comp_sem.at[part],
        )
        for part in range(comp_parts)
    ]
    for item in loads_comp:
        item.start()
    barrier = pltpu.get_barrier_semaphore()
    for target in [sibling] + partners:
        pl.semaphore_signal(barrier, inc=1, device_id=target, device_id_type=MESH)
    tables = ((pairs_h, pairs_s), (order_h, order_s))
    loads_tables = [pltpu.make_async_copy(*tables[i], table_sem.at[i]) for i in range(len(tables))]
    for item in loads_tables:
        item.start()
    factors = (la_h, lb_h)
    loads_lev = [pltpu.make_async_copy(factors[ab], lev_v.at[ab, tgt], lev_sem.at[ab]) for ab in range(2)]
    for item in loads_lev:
        item.start()
    loads_tiles = [
        pltpu.make_async_copy(
            tiles_h.at[pl.ds(part * slots_part, slots_part)],
            tiles_v.at[pl.ds(part * slots_part, slots_part)],
            tiles_sem.at[part],
        )
        for part in range(tile_parts)
    ]
    loads_exp = [pltpu.make_async_copy(exp_h.at[:, c], expt_v.at[c], exp_sem.at[c]) for c in range(clusters)]
    turns_exp = [
        pltpu.make_async_copy(expt_v.at[c].reshape(2 * rank, width), exp_v.at[c], expt_sem.at[c])
        for c in range(clusters)
    ]

    upper_c, lower_c = spread(width, True)
    upper, lower = spread(width, False)

    pl.semaphore_wait(barrier, 1 + levels)
    swaps_lev = [
        [
            pltpu.make_async_remote_copy(
                src_ref=factors[ab].at[level], dst_ref=lev_v.at[ab, tgt, level],
                send_sem=levs_sem.at[ab, level], recv_sem=levr_sem.at[ab, level],
                device_id=sibling, device_id_type=MESH,
            )
            for ab in range(2)
        ]
        for level in range(levels)
    ]
    for item in swaps_lev[0]:
        item.start()

    per_part = clusters // comp_parts

    def dens_half(h, c):
        cut = pl.ds(c * width, width)
        real = dens_v[pl.ds(pl.multiple_of(h * half, half), half), cut]
        imag = dens_v[pl.ds(pl.multiple_of(rhs + h * half, half), half), cut]
        return jnp.concatenate([real, imag], axis=1)

    def lift_half(h):
        for part in range(comp_parts):
            members = range(part * per_part, (part + 1) * per_part)
            stacked = jnp.concatenate([dens_half(h, c) for c in members], axis=0)
            above = matmul(stacked, upper_c).astype(BF16)
            below = matmul(stacked, lower_c).astype(BF16)
            for i, c in enumerate(members):
                cut = pl.ds(c * 2 * width, 2 * width)
                liftc_v[0:half, cut] = above[i * half : (i + 1) * half]
                liftc_v[half : 2 * half, cut] = below[i * half : (i + 1) * half]

    def split(part):
        depth = 2 * lanes * width
        even = (lax.broadcasted_iota(jnp.int32, (depth // 32, 16, width), 1) // 2) % 2 == 0
        for c in range(part * per_part, (part + 1) * per_part):
            block = comp_v[pl.ds(c * depth, depth)].reshape(depth // 32, 2, 16, width)
            first, second = block[:, 0], block[:, 1]
            left = jnp.where(even, first, pltpu.roll(second, 2, 1))
            right = jnp.where(even, pltpu.roll(first, 14, 1), second)
            compd_v[pl.ds(c * 2 * width, 2 * width), pl.ds(0, width)] = left.reshape(2 * width, width)
            compd_v[pl.ds(c * 2 * width, 2 * width), pl.ds(width, width)] = right.reshape(2 * width, width)

    def squeeze(part):
        cut = pl.ds(part * per_part * 2 * width, per_part * 2 * width)
        return matmul(liftc_v[:, cut], compd_v[cut])

    loads_dens.wait()
    lift_half(other)
    total = jnp.zeros((2 * half, rank), F32)
    for part in range(comp_parts):
        loads_comp[part].wait()
        split(part)
        total = total + squeeze(part)
    part_v[...] = total.astype(BF16)
    swap_part = pltpu.make_async_remote_copy(
        src_ref=part_v, dst_ref=part_r, send_sem=part_sem.at[0], recv_sem=part_sem.at[1],
        device_id=sibling, device_id_type=MESH,
    )
    swap_part.start()
    for item in loads_tiles:
        item.start()
    for item in loads_exp:
        item.start()
    for level in range(1, levels):
        for item in swaps_lev[level]:
            item.start()
    lift_half(tgt)
    total = jnp.zeros((2 * half, rank), F32)
    for part in range(comp_parts):
        total = total + squeeze(part)

    def prepare(level):
        for ab in range(2):
            if level == 0:
                loads_lev[ab].wait()
            swaps_lev[level][ab].wait()
            whole = jnp.concatenate([lev_v[ab, h, level] for h in range(n_tgt)], axis=1)
            for lane in range(lanes):
                block = whole[lane * 2 * width : (lane + 1) * 2 * width]
                turned = lax.dot_general(
                    gather_m, block, (((1,), (0,)), ((), ())), preferred_element_type=F32
                )
                real, imag = turned[:width].astype(BF16), turned[width:].astype(BF16)
                top, bottom = pl.ds(lane * width, width), pl.ds(rank + lane * width, width)
                big_v[ab, level, top, pl.ds(0, rank)] = real
                big_v[ab, level, top, pl.ds(rank, rank)] = imag
                big_v[ab, level, bottom, pl.ds(0, rank)] = -imag
                big_v[ab, level, bottom, pl.ds(rank, rank)] = real

    row = lax.broadcasted_iota(jnp.int32, (2 * width, 2 * width), 0)
    col = lax.broadcasted_iota(jnp.int32, (2 * width, 2 * width), 1)
    spot = jnp.where(row < width, 2 * row, 2 * (row - width) + 1)
    gather_m = jnp.where(spot == col, jnp.ones(row.shape, F32), jnp.zeros(row.shape, F32)).astype(BF16)

    def send(level, q):
        copy = pltpu.make_async_remote_copy(
            src_ref=coef_v.at[level, q], dst_ref=recv_v.at[level, q],
            send_sem=send_sem.at[level, q], recv_sem=recv_sem.at[level, q],
            device_id=partners[level], device_id_type=MESH,
        )
        copy.start()
        return copy

    for item in loads_tables:
        item.wait()
    count = count_s[0]
    last = [jnp.int32(slots) for _ in range(clusters)]
    sums_v[slots] = jnp.zeros((2 * rhs, width), F32)

    def near_step(step, last):
        last = list(last)
        base = step * UNROLL
        terms = [matmul(lifted_v[pairs_s[1, base + u]], tiles_v[base + u]) for u in range(UNROLL)]
        for u in range(UNROLL):
            slot = base + u
            target = pairs_s[0, slot]
            active = slot < count
            before = jnp.int32(slots)
            for c in range(clusters):
                hit = target == c
                before = jnp.where(hit, last[c], before)
                last[c] = jnp.where(hit & active, slot, last[c])
            sums_v[slot] = terms[u] + sums_v[before]
        return tuple(last)

    prepare(0)
    swap_part.wait()
    sends = []
    for q in range(CHUNKS):
        real = total[q * rows : (q + 1) * rows] + part_r[pl.ds(q * rows, rows)].astype(F32)
        imag = total[half + q * rows : half + (q + 1) * rows] + part_r[pl.ds(half + q * rows, rows)].astype(F32)
        coef_v[0, q] = jnp.concatenate([real, imag], axis=1).astype(BF16)
        sends.append(send(0, q))

    for c in range(clusters):
        cut = pl.ds(c * width, width)
        both = jnp.concatenate([dens_v[:rhs, cut], dens_v[rhs:, cut]], axis=1)
        lifted_v[c, :rhs] = matmul(both, upper).astype(BF16)
        lifted_v[c, rhs:] = matmul(both, lower).astype(BF16)

    current = sends
    done_sends = []
    swaps_fin = []
    for level in range(levels):
        own = matmul(
            jnp.concatenate([coef_v[level, q] for q in range(CHUNKS)], axis=0), big_v[0, level]
        )
        if level + 1 < levels:
            prepare(level + 1)
        first, final = (tile_parts * level) // levels, (tile_parts * (level + 1)) // levels
        for part in range(first, final):
            loads_tiles[part].wait()
        last = lax.fori_loop(
            first * slots_part // UNROLL, final * slots_part // UNROLL, near_step, tuple(last)
        )
        if level + 1 == levels:
            for item in turns_exp:
                item.wait()
        elif level + 2 == levels:
            for c in range(clusters):
                loads_exp[c].wait()
                turns_exp[c].start()
        following = []
        for q in range(CHUNKS):
            current[q].wait_recv()
            fresh = own[q * rows : (q + 1) * rows] + matmul(recv_v[level, q], big_v[1, level])
            coef_v[level + 1, q] = fresh.astype(BF16)
            if level + 1 < levels:
                following.append(send(level + 1, q))
            else:
                copy = pltpu.make_async_remote_copy(
                    src_ref=coef_v.at[levels, q], dst_ref=fin_r.at[q],
                    send_sem=fin_sem.at[0, q], recv_sem=fin_sem.at[1, q],
                    device_id=sibling, device_id_type=MESH,
                )
                copy.start()
                swaps_fin.append(copy)
        done_sends += current
        current = following

    origins = []
    for t in range(clusters):
        origin = jnp.int32(0)
        for c in range(clusters):
            origin = jnp.where(order_s[0, c] == t, c, origin)
        origins.append(origin)

    def finish(h, whole):
        pieces = [
            jnp.concatenate(
                [whole[:, lane * width : (lane + 1) * width], whole[:, rank + lane * width : rank + (lane + 1) * width]],
                axis=1,
            )
            for lane in range(lanes)
        ]
        operand = jnp.concatenate(
            [
                jnp.concatenate([matmul(piece, side).astype(BF16) for piece in pieces], axis=1)
                for side in (upper, lower)
            ],
            axis=0,
        )
        top = pl.ds(pl.multiple_of(h * half, half), half)
        bottom = pl.ds(pl.multiple_of(rhs + h * half, half), half)
        for t in range(0, clusters, 2):
            pair = jnp.concatenate([exp_v[origins[t]], exp_v[origins[t + 1]]], axis=1)
            far = matmul(operand, pair)
            for u in range(2):
                cut = pl.ds((t + u) * width, width)
                side = far[:, u * width : (u + 1) * width]
                out_v[top, cut] = (side[:half] + sums_v[last[t + u], top]).astype(BF16)
                out_v[bottom, cut] = (side[half:] + sums_v[last[t + u], bottom]).astype(BF16)

    finish(tgt, jnp.concatenate([coef_v[levels, q] for q in range(CHUNKS)], axis=0))
    for item in swaps_fin:
        item.wait()
    finish(other, jnp.concatenate([fin_r[q] for q in range(CHUNKS)], axis=0))
    for item in done_sends:
        item.wait_send()


def shards(
    densities, compress, level_a, level_b, expand, near_tiles, tile_pairs, tile_count, cluster_order
):
    row_count, points = densities.shape
    rhs = row_count // 2
    rank = compress.shape[2]
    levels = level_a.shape[0]
    clusters = cluster_order.shape[1]
    width = points // clusters
    slots = near_tiles.shape[0]
    n_tgt = lax.axis_size("tgt")
    sizes = (levels, clusters, width, slots, rhs, rank, n_tgt)
    lanes = rank // width
    assert lanes == 2 and n_tgt == 2
    half = rhs // n_tgt
    rows = half // CHUNKS
    comp_parts, tile_parts = 4, 16
    anywhere = pl.BlockSpec(memory_space=pl.ANY)
    dma = pltpu.SemaphoreType.DMA
    operands = (
        densities,
        compress.reshape(points, 2, lanes, width).transpose(0, 2, 1, 3).reshape(points * lanes * 2, width),
        level_a.reshape(levels, rank * 2, width),
        level_b.reshape(levels, rank * 2, width),
        expand.reshape(rank, 2, clusters, width).transpose(0, 2, 1, 3),
        near_tiles.reshape(slots, width * 2, width),
    )
    tables = (tile_pairs.T, cluster_order)
    operands = [pltpu.with_memory_space_constraint(item, pltpu.HBM) for item in operands]
    tables = [pltpu.with_memory_space_constraint(item, pltpu.HBM) for item in tables]
    return pl.pallas_call(
        functools.partial(kernel, sizes),
        out_shape=jax.ShapeDtypeStruct((row_count, points), BF16),
        in_specs=[anywhere] * 8 + [pl.BlockSpec(memory_space=pltpu.SMEM)],
        out_specs=pl.BlockSpec(memory_space=pltpu.VMEM),
        scratch_shapes=[
            pltpu.VMEM((row_count, points), BF16),
            pltpu.VMEM((points * lanes * 2, width), BF16),
            pltpu.VMEM((points * 2, rank), BF16),
            pltpu.VMEM((2, n_tgt, levels, rank * 2, width), BF16),
            pltpu.VMEM((2, levels, rank * 2, rank * 2), BF16),
            pltpu.VMEM((clusters, rank, 2, width), BF16),
            pltpu.VMEM((clusters, rank * 2, width), BF16),
            pltpu.VMEM((slots, width * 2, width), BF16),
            pltpu.VMEM((row_count // n_tgt, points * 2), BF16),
            pltpu.VMEM((clusters, row_count, 2 * width), BF16),
            pltpu.VMEM((slots + 1, row_count, width), F32),
            pltpu.VMEM((row_count // n_tgt, rank), BF16),
            pltpu.VMEM((row_count // n_tgt, rank), BF16),
            pltpu.VMEM((levels + 1, CHUNKS, rows, 2 * rank), BF16),
            pltpu.VMEM((levels, CHUNKS, rows, 2 * rank), BF16),
            pltpu.VMEM((CHUNKS, rows, 2 * rank), BF16),
            pltpu.SMEM((2, slots), jnp.int32),
            pltpu.SMEM((1, clusters), jnp.int32),
            dma,
            dma((comp_parts,)),
            dma((2,)),
            dma((2, levels)),
            dma((2, levels)),
            dma((clusters,)),
            dma((clusters,)),
            dma((tile_parts,)),
            dma((2,)),
            dma((levels, CHUNKS)),
            dma((levels, CHUNKS)),
            dma((2, CHUNKS)),
            dma((2,)),
        ],
        compiler_params=pltpu.CompilerParams(
            collective_id=0, has_side_effects=True, vmem_limit_bytes=48 << 20
        ),
    )(*operands, *tables, tile_count)


def solution(mesh):
    placed = (
        P("grp", ("src", "tgt")),
        P(("grp", "src", "tgt"), None, None),
        P("grp", "src", None, "tgt"),
        P("grp", "src", None, "tgt"),
        P(("grp", "src"), None, "tgt"),
        P(("grp", "src", "tgt"), None, None, None),
        P(("grp", "src", "tgt"), None),
        P(("grp", "src", "tgt")),
        P(("grp", "src", "tgt"), None),
    )
    return jax.shard_map(
        shards, mesh=mesh, in_specs=placed, out_specs=P("grp", ("src", "tgt")), check_vma=False
    )
```

time: 28.1 us -> 24.5 us (0.87)
  Pallas kernels: 25 us -> 22.8 us
  local copies, waits for them, and re-layouts: 2.3 us -> 0.97 us
    pallas_call x1, Pallas kernels: 25 us -> 22.8 us  [shards(): pl.pallas_call(functools.partial(kernel, sizes), out_shape=jax.ShapeDtype...]
    unnamed x1, local copies, waits for them, and re-layouts: 2.3 us -> 0.97 us
where the time goes in v1:
time: 24.5 us; the launch traced here: 24.4 us
  Pallas kernels  22.8 us (93%)
  local copies, waits for them, and re-layouts  0.97 us (4%)
  between operations  0.66 us (3%)
    pallas_call x1, Pallas kernels, shards(): pl.pallas_call(functools.partial(kernel, sizes), out_shape=jax.ShapeDtype...  22.8 us
    unnamed x1, local copies, waits for them, and re-layouts  0.97 us

profile of v1, /device:TPU:0, one launch (start us, length us, event | category | flops | bytes accessed | tf_op | source)
XLA Modules:
  0.0 24.4 jit_solution(3571547523195653044)
XLA Ops:
  0.7 22.8 %shard_map.91 = bf16[256,2048]{1,0:T(8,128)(2,1)S(1)} custom-call(bf16[256,2048]{1,0:T(8,128)(2,1)} %dens_h.1, bf16[8192,128]{1,0:T(8,128)(2,1)} %bitcast.13, bf16[3,512,128]{2,1,0:T(8,128)(2,1)} %bitcast.15, bf16[3,512,128]{2,1,0:T(8,128)(2,1)} %bitcast.16, bf16[256,16,2,128]{3,2,1,0:T(2,128)(2,1)} %bitcast.14, bf16[64,256,128]{2,1,0:T(8,128)(2,1)} %bitcast.12, ...), custom_call_target="tpu_custom_call" | custom-call | tf_op jit(solution)/shard_map/pallas_call | solution.py:350
  23.4 1.0 %copy.13 = bf16[256,2048]{1,0:T(8,128)(2,1)} copy(bf16[256,2048]{1,0:T(8,128)(2,1)S(1)} %shard_map.91) | data formatting | bytes 2097152

commit v2 on v1

--- a/solution.py
+++ b/solution.py
@@ -17,26 +17,28 @@
     return jnp.dot(a, b, preferred_element_type=F32)
 
 
-def spread(width, grouped):
+def spread(width):
     row = lax.broadcasted_iota(jnp.int32, (2 * width, 2 * width), 0)
     col = lax.broadcasted_iota(jnp.int32, (2 * width, 2 * width), 1)
     imag = row >= width
     point = jnp.where(imag, row - width, row)
-    if grouped:
-        within = point & 7
-        point = (point - within) + jnp.where(within < 4, 2 * within, 2 * within - 7)
     one, zero = jnp.ones(row.shape, F32), jnp.zeros(row.shape, F32)
-    signed = jnp.where(imag, -one, one)
-    upper = jnp.where(jnp.where(imag, 2 * point + 1, 2 * point) == col, signed, zero)
+    upper = jnp.where(jnp.where(imag, 2 * point + 1, 2 * point) == col, jnp.where(imag, -one, one), zero)
     lower = jnp.where(jnp.where(imag, 2 * point, 2 * point + 1) == col, one, zero)
     return upper.astype(BF16), lower.astype(BF16)
+
+
+def joined(real, imag):
+    top = jnp.concatenate([real, imag], axis=1)
+    bottom = jnp.concatenate([-imag, real], axis=1)
+    return jnp.concatenate([top, bottom], axis=0)
 
 
 def kernel(
     sizes,
     dens_h, comp_h, la_h, lb_h, exp_h, tiles_h, pairs_h, order_h, count_s,
     out_v,
-    dens_v, comp_v, compd_v, lev_v, big_v, expt_v, exp_v, tiles_v, liftc_v, lifted_v, sums_v,
+    dens_v, comp_v, compd_v, lev_v, big_v, expt_v, exp_v, tiles_v, wide_v, point_v, sums_v,
     part_v, part_r, coef_v, recv_v, fin_r, pairs_s, order_s,
     dens_sem, comp_sem, lev_sem, levs_sem, levr_sem, exp_sem, expt_sem, tiles_sem, part_sem, send_sem, recv_sem,
     fin_sem, table_sem,
@@ -84,16 +86,14 @@
         )
         for part in range(tile_parts)
     ]
-    loads_exp = [pltpu.make_async_copy(exp_h.at[:, c], expt_v.at[c], exp_sem.at[c]) for c in range(clusters)]
+    loads_exp = [pltpu.make_async_copy(exp_h.at[:, c], expt_v.at[c], exp_sem) for c in range(clusters)]
     turns_exp = [
-        pltpu.make_async_copy(expt_v.at[c].reshape(2 * rank, width), exp_v.at[c], expt_sem.at[c])
+        pltpu.make_async_copy(expt_v.at[c].reshape(2 * rank, width), exp_v.at[c], expt_sem)
         for c in range(clusters)
     ]
-
-    upper_c, lower_c = spread(width, True)
-    upper, lower = spread(width, False)
-
-    pl.semaphore_wait(barrier, 1 + levels)
+    all_exp = pltpu.make_async_copy(expt_v, expt_v, exp_sem)
+    all_turns = pltpu.make_async_copy(exp_v, exp_v, expt_sem)
+
     swaps_lev = [
         [
             pltpu.make_async_remote_copy(
@@ -105,90 +105,74 @@
         ]
         for level in range(levels)
     ]
-    for item in swaps_lev[0]:
-        item.start()
 
     per_part = clusters // comp_parts
 
-    def dens_half(h, c):
+    def parts(buffer, stride, offset):
+        return wide_v[buffer, pl.ds(offset, width, stride=stride), :].astype(BF16)
+
+    def split(c):
+        depth = 2 * lanes * width
+        wide_v[c % UNROLL] = comp_v[pl.ds(c * depth, depth)].astype(F32)
+        for lane in range(lanes):
+            for ri in range(2):
+                compd_v[c, :, pl.ds(ri * rank + lane * width, width)] = parts(c % UNROLL, 2 * lanes, 2 * lane + ri)
+
+    def squeeze(part, h):
+        members = range(part * per_part, (part + 1) * per_part)
+        cut = pl.ds(pl.multiple_of(h * half, half), half)
+        left = jnp.concatenate([point_v[c, cut] for c in members], axis=1)
+        right = jnp.concatenate([joined(compd_v[c, :, :rank], compd_v[c, :, rank:]) for c in members], axis=0)
+        return matmul(left, right)
+
+    loads_dens.wait()
+    for c in range(clusters):
         cut = pl.ds(c * width, width)
-        real = dens_v[pl.ds(pl.multiple_of(h * half, half), half), cut]
-        imag = dens_v[pl.ds(pl.multiple_of(rhs + h * half, half), half), cut]
-        return jnp.concatenate([real, imag], axis=1)
-
-    def lift_half(h):
-        for part in range(comp_parts):
-            members = range(part * per_part, (part + 1) * per_part)
-            stacked = jnp.concatenate([dens_half(h, c) for c in members], axis=0)
-            above = matmul(stacked, upper_c).astype(BF16)
-            below = matmul(stacked, lower_c).astype(BF16)
-            for i, c in enumerate(members):
-                cut = pl.ds(c * 2 * width, 2 * width)
-                liftc_v[0:half, cut] = above[i * half : (i + 1) * half]
-                liftc_v[half : 2 * half, cut] = below[i * half : (i + 1) * half]
-
-    def split(part):
-        depth = 2 * lanes * width
-        even = (lax.broadcasted_iota(jnp.int32, (depth // 32, 16, width), 1) // 2) % 2 == 0
-        for c in range(part * per_part, (part + 1) * per_part):
-            block = comp_v[pl.ds(c * depth, depth)].reshape(depth // 32, 2, 16, width)
-            first, second = block[:, 0], block[:, 1]
-            left = jnp.where(even, first, pltpu.roll(second, 2, 1))
-            right = jnp.where(even, pltpu.roll(first, 14, 1), second)
-            compd_v[pl.ds(c * 2 * width, 2 * width), pl.ds(0, width)] = left.reshape(2 * width, width)
-            compd_v[pl.ds(c * 2 * width, 2 * width), pl.ds(width, width)] = right.reshape(2 * width, width)
-
-    def squeeze(part):
-        cut = pl.ds(part * per_part * 2 * width, per_part * 2 * width)
-        return matmul(liftc_v[:, cut], compd_v[cut])
-
-    loads_dens.wait()
-    lift_half(other)
-    total = jnp.zeros((2 * half, rank), F32)
+        point_v[c, :, :width] = dens_v[:rhs, cut]
+        point_v[c, :, width:] = dens_v[rhs:, cut]
+    total = jnp.zeros((half, 2 * rank), F32)
     for part in range(comp_parts):
         loads_comp[part].wait()
-        split(part)
-        total = total + squeeze(part)
+        for c in range(part * per_part, (part + 1) * per_part):
+            split(c)
+        total = total + squeeze(part, other)
     part_v[...] = total.astype(BF16)
     swap_part = pltpu.make_async_remote_copy(
         src_ref=part_v, dst_ref=part_r, send_sem=part_sem.at[0], recv_sem=part_sem.at[1],
         device_id=sibling, device_id_type=MESH,
     )
+    pl.semaphore_wait(barrier, 1 + levels)
     swap_part.start()
-    for item in loads_tiles:
-        item.start()
-    for item in loads_exp:
-        item.start()
-    for level in range(1, levels):
+    for level in range(levels):
         for item in swaps_lev[level]:
             item.start()
-    lift_half(tgt)
-    total = jnp.zeros((2 * half, rank), F32)
+    for item in loads_tiles:
+        item.start()
+    for item in loads_exp:
+        item.start()
+    total = jnp.zeros((half, 2 * rank), F32)
     for part in range(comp_parts):
-        total = total + squeeze(part)
+        total = total + squeeze(part, tgt)
 
     def prepare(level):
         for ab in range(2):
             if level == 0:
                 loads_lev[ab].wait()
             swaps_lev[level][ab].wait()
-            whole = jnp.concatenate([lev_v[ab, h, level] for h in range(n_tgt)], axis=1)
-            for lane in range(lanes):
-                block = whole[lane * 2 * width : (lane + 1) * 2 * width]
-                turned = lax.dot_general(
-                    gather_m, block, (((1,), (0,)), ((), ())), preferred_element_type=F32
-                )
-                real, imag = turned[:width].astype(BF16), turned[width:].astype(BF16)
-                top, bottom = pl.ds(lane * width, width), pl.ds(rank + lane * width, width)
-                big_v[ab, level, top, pl.ds(0, rank)] = real
-                big_v[ab, level, top, pl.ds(rank, rank)] = imag
-                big_v[ab, level, bottom, pl.ds(0, rank)] = -imag
-                big_v[ab, level, bottom, pl.ds(rank, rank)] = real
-
-    row = lax.broadcasted_iota(jnp.int32, (2 * width, 2 * width), 0)
-    col = lax.broadcasted_iota(jnp.int32, (2 * width, 2 * width), 1)
-    spot = jnp.where(row < width, 2 * row, 2 * (row - width) + 1)
-    gather_m = jnp.where(spot == col, jnp.ones(row.shape, F32), jnp.zeros(row.shape, F32)).astype(BF16)
+            for h in range(n_tgt):
+                cells = [[None] * 2 for _ in range(lanes)]
+                wide_v[2 * ab + h] = lev_v[ab, h, level].astype(F32)
+                for block in range(lanes):
+                    for ri in range(2):
+                        cells[block][ri] = parts(2 * ab + h, 2, block * 2 * width + ri)
+                for block in range(lanes):
+                    real, imag = cells[block]
+                    top, bottom = pl.ds(block * width, width), pl.ds(rank + block * width, width)
+                    left, right = pl.ds(h * width, width), pl.ds(rank + h * width, width)
+                    big_v[ab, level, top, left] = real
+                    big_v[ab, level, top, right] = imag
+                    big_v[ab, level, bottom, left] = -imag
+                    big_v[ab, level, bottom, right] = real
 
     def send(level, q):
         copy = pltpu.make_async_remote_copy(
@@ -203,12 +187,15 @@
         item.wait()
     count = count_s[0]
     last = [jnp.int32(slots) for _ in range(clusters)]
-    sums_v[slots] = jnp.zeros((2 * rhs, width), F32)
+    sums_v[slots] = jnp.zeros((rhs, 2 * width), F32)
 
     def near_step(step, last):
         last = list(last)
         base = step * UNROLL
-        terms = [matmul(lifted_v[pairs_s[1, base + u]], tiles_v[base + u]) for u in range(UNROLL)]
+        terms = []
+        for u in range(UNROLL):
+            wide_v[u, pl.ds(0, 2 * width), :] = tiles_v[base + u].astype(F32)
+            terms.append(matmul(point_v[pairs_s[1, base + u]], joined(parts(u, 2, 0), parts(u, 2, 1))))
         for u in range(UNROLL):
             slot = base + u
             target = pairs_s[0, slot]
@@ -225,17 +212,11 @@
     swap_part.wait()
     sends = []
     for q in range(CHUNKS):
-        real = total[q * rows : (q + 1) * rows] + part_r[pl.ds(q * rows, rows)].astype(F32)
-        imag = total[half + q * rows : half + (q + 1) * rows] + part_r[pl.ds(half + q * rows, rows)].astype(F32)
-        coef_v[0, q] = jnp.concatenate([real, imag], axis=1).astype(BF16)
+        cut = pl.ds(q * rows, rows)
+        coef_v[0, q] = (total[q * rows : (q + 1) * rows] + part_r[cut].astype(F32)).astype(BF16)
         sends.append(send(0, q))
 
-    for c in range(clusters):
-        cut = pl.ds(c * width, width)
-        both = jnp.concatenate([dens_v[:rhs, cut], dens_v[rhs:, cut]], axis=1)
-        lifted_v[c, :rhs] = matmul(both, upper).astype(BF16)
-        lifted_v[c, rhs:] = matmul(both, lower).astype(BF16)
-
+    upper, lower = spread(width)
     current = sends
     done_sends = []
     swaps_fin = []
@@ -252,12 +233,11 @@
             first * slots_part // UNROLL, final * slots_part // UNROLL, near_step, tuple(last)
         )
         if level + 1 == levels:
+            all_turns.wait()
+        elif level + 2 == levels:
+            all_exp.wait()
             for item in turns_exp:
-                item.wait()
-        elif level + 2 == levels:
-            for c in range(clusters):
-                loads_exp[c].wait()
-                turns_exp[c].start()
+                item.start()
         following = []
         for q in range(CHUNKS):
             current[q].wait_recv()
@@ -306,15 +286,15 @@
             for u in range(2):
                 cut = pl.ds((t + u) * width, width)
                 side = far[:, u * width : (u + 1) * width]
-                out_v[top, cut] = (side[:half] + sums_v[last[t + u], top]).astype(BF16)
-                out_v[bottom, cut] = (side[half:] + sums_v[last[t + u], bottom]).astype(BF16)
+                out_v[top, cut] = (side[:half] + sums_v[last[t + u], top, :width]).astype(BF16)
+                out_v[bottom, cut] = (side[half:] + sums_v[last[t + u], top, width:]).astype(BF16)
 
     finish(tgt, jnp.concatenate([coef_v[levels, q] for q in range(CHUNKS)], axis=0))
+    for item in done_sends:
+        item.wait_send()
     for item in swaps_fin:
         item.wait()
     finish(other, jnp.concatenate([fin_r[q] for q in range(CHUNKS)], axis=0))
-    for item in done_sends:
-        item.wait_send()
 
 
 def shards(
@@ -330,10 +310,10 @@
     n_tgt = lax.axis_size("tgt")
     sizes = (levels, clusters, width, slots, rhs, rank, n_tgt)
     lanes = rank // width
-    assert lanes == 2 and n_tgt == 2
+    assert lanes == 2 and n_tgt == 2 and UNROLL >= 2 * n_tgt
     half = rhs // n_tgt
     rows = half // CHUNKS
-    comp_parts, tile_parts = 4, 16
+    comp_parts, tile_parts = 4, 8
     anywhere = pl.BlockSpec(memory_space=pl.ANY)
     dma = pltpu.SemaphoreType.DMA
     operands = (
@@ -355,17 +335,17 @@
         scratch_shapes=[
             pltpu.VMEM((row_count, points), BF16),
             pltpu.VMEM((points * lanes * 2, width), BF16),
-            pltpu.VMEM((points * 2, rank), BF16),
+            pltpu.VMEM((clusters, width, 2 * rank), BF16),
             pltpu.VMEM((2, n_tgt, levels, rank * 2, width), BF16),
             pltpu.VMEM((2, levels, rank * 2, rank * 2), BF16),
             pltpu.VMEM((clusters, rank, 2, width), BF16),
             pltpu.VMEM((clusters, rank * 2, width), BF16),
             pltpu.VMEM((slots, width * 2, width), BF16),
-            pltpu.VMEM((row_count // n_tgt, points * 2), BF16),
-            pltpu.VMEM((clusters, row_count, 2 * width), BF16),
-            pltpu.VMEM((slots + 1, row_count, width), F32),
-            pltpu.VMEM((row_count // n_tgt, rank), BF16),
-            pltpu.VMEM((row_count // n_tgt, rank), BF16),
+            pltpu.VMEM((UNROLL, width * 2 * lanes, width), F32),
+            pltpu.VMEM((clusters, rhs, 2 * width), BF16),
+            pltpu.VMEM((slots + 1, rhs, 2 * width), F32),
+            pltpu.VMEM((half, 2 * rank), BF16),
+            pltpu.VMEM((half, 2 * rank), BF16),
             pltpu.VMEM((levels + 1, CHUNKS, rows, 2 * rank), BF16),
             pltpu.VMEM((levels, CHUNKS, rows, 2 * rank), BF16),
             pltpu.VMEM((CHUNKS, rows, 2 * rank), BF16),
@@ -376,8 +356,8 @@
             dma((2,)),
             dma((2, levels)),
             dma((2, levels)),
-            dma((clusters,)),
-            dma((clusters,)),
+            dma,
+            dma,
             dma((tile_parts,)),
             dma((2,)),
             dma((levels, CHUNKS)),

time: 24.5 us -> 25.7 us (1.049)
  Pallas kernels: 22.8 us -> 23.9 us
    pallas_call x1, Pallas kernels: 22.8 us -> 23.9 us  [shards(): pl.pallas_call(functools.partial(kernel, sizes), out_shape=jax.ShapeDtype...]
where the time goes in v2:
time: 25.7 us; the launch traced here: 25.5 us
  Pallas kernels  23.9 us (93%)
  local copies, waits for them, and re-layouts  0.97 us (4%)
  between operations  0.66 us (3%)
    pallas_call x1, Pallas kernels, shards(): pl.pallas_call(functools.partial(kernel, sizes), out_shape=jax.ShapeDtype...  23.9 us
    unnamed x1, local copies, waits for them, and re-layouts  0.97 us

profile of v2, /device:TPU:0, one launch (start us, length us, event | category | flops | bytes accessed | tf_op | source)
XLA Modules:
  0.0 25.5 jit_solution(4589976762736253475)
XLA Ops:
  0.7 23.9 %shard_map.91 = bf16[256,2048]{1,0:T(8,128)(2,1)S(1)} custom-call(bf16[256,2048]{1,0:T(8,128)(2,1)} %dens_h.1, bf16[8192,128]{1,0:T(8,128)(2,1)} %bitcast.13, bf16[3,512,128]{2,1,0:T(8,128)(2,1)} %bitcast.15, bf16[3,512,128]{2,1,0:T(8,128)(2,1)} %bitcast.16, bf16[256,16,2,128]{3,2,1,0:T(2,128)(2,1)} %bitcast.14, bf16[64,256,128]{2,1,0:T(8,128)(2,1)} %bitcast.12, ...), custom_call_target="tpu_custom_call" | custom-call | tf_op jit(solution)/shard_map/pallas_call | solution.py:330
  24.5 1.0 %copy.13 = bf16[256,2048]{1,0:T(8,128)(2,1)} copy(bf16[256,2048]{1,0:T(8,128)(2,1)S(1)} %shard_map.91) | data formatting | bytes 2097152

commit v3 on v2

--- a/solution.py
+++ b/solution.py
@@ -8,8 +8,8 @@
 from jax.sharding import PartitionSpec as P
 
 MESH = pl.DeviceIdType.MESH
-CHUNKS = 2
-UNROLL = 4
+CHUNKS = 4
+UNROLL = 8
 BF16, F32 = jnp.bfloat16, jnp.float32
 
 
@@ -106,6 +106,10 @@
         for level in range(levels)
     ]
 
+    for item in loads_tiles:
+        item.start()
+    for item in loads_exp:
+        item.start()
     per_part = clusters // comp_parts
 
     def parts(buffer, stride, offset):
@@ -121,15 +125,14 @@
     def squeeze(part, h):
         members = range(part * per_part, (part + 1) * per_part)
         cut = pl.ds(pl.multiple_of(h * half, half), half)
-        left = jnp.concatenate([point_v[c, cut] for c in members], axis=1)
+        below = pl.ds(pl.multiple_of(rhs + h * half, half), half)
+        left = jnp.concatenate(
+            [dens_v[side, pl.ds(c * width, width)] for c in members for side in (cut, below)], axis=1
+        )
         right = jnp.concatenate([joined(compd_v[c, :, :rank], compd_v[c, :, rank:]) for c in members], axis=0)
         return matmul(left, right)
 
     loads_dens.wait()
-    for c in range(clusters):
-        cut = pl.ds(c * width, width)
-        point_v[c, :, :width] = dens_v[:rhs, cut]
-        point_v[c, :, width:] = dens_v[rhs:, cut]
     total = jnp.zeros((half, 2 * rank), F32)
     for part in range(comp_parts):
         loads_comp[part].wait()
@@ -146,10 +149,6 @@
     for level in range(levels):
         for item in swaps_lev[level]:
             item.start()
-    for item in loads_tiles:
-        item.start()
-    for item in loads_exp:
-        item.start()
     total = jnp.zeros((half, 2 * rank), F32)
     for part in range(comp_parts):
         total = total + squeeze(part, tgt)
@@ -208,7 +207,6 @@
             sums_v[slot] = terms[u] + sums_v[before]
         return tuple(last)
 
-    prepare(0)
     swap_part.wait()
     sends = []
     for q in range(CHUNKS):
@@ -216,28 +214,29 @@
         coef_v[0, q] = (total[q * rows : (q + 1) * rows] + part_r[cut].astype(F32)).astype(BF16)
         sends.append(send(0, q))
 
+    for c in range(clusters):
+        cut = pl.ds(c * width, width)
+        point_v[c, :, :width] = dens_v[:rhs, cut]
+        point_v[c, :, width:] = dens_v[rhs:, cut]
     upper, lower = spread(width)
     current = sends
     done_sends = []
     swaps_fin = []
     for level in range(levels):
+        prepare(level)
         own = matmul(
             jnp.concatenate([coef_v[level, q] for q in range(CHUNKS)], axis=0), big_v[0, level]
         )
-        if level + 1 < levels:
-            prepare(level + 1)
         first, final = (tile_parts * level) // levels, (tile_parts * (level + 1)) // levels
+        if level + 1 == levels:
+            all_exp.wait()
+            for item in turns_exp:
+                item.start()
         for part in range(first, final):
             loads_tiles[part].wait()
         last = lax.fori_loop(
             first * slots_part // UNROLL, final * slots_part // UNROLL, near_step, tuple(last)
         )
-        if level + 1 == levels:
-            all_turns.wait()
-        elif level + 2 == levels:
-            all_exp.wait()
-            for item in turns_exp:
-                item.start()
         following = []
         for q in range(CHUNKS):
             current[q].wait_recv()
@@ -289,6 +288,7 @@
                 out_v[top, cut] = (side[:half] + sums_v[last[t + u], top, :width]).astype(BF16)
                 out_v[bottom, cut] = (side[half:] + sums_v[last[t + u], top, width:]).astype(BF16)
 
+    all_turns.wait()
     finish(tgt, jnp.concatenate([coef_v[levels, q] for q in range(CHUNKS)], axis=0))
     for item in done_sends:
         item.wait_send()

time: 25.7 us -> 22.2 us (0.86)
  Pallas kernels: 23.9 us -> 20.4 us
    pallas_call x1, Pallas kernels: 23.9 us -> 20.4 us  [shards(): pl.pallas_call(functools.partial(kernel, sizes), out_shape=jax.ShapeDtype...]
where the time goes in v3:
time: 22.2 us; the launch traced here: 22 us
  Pallas kernels  20.4 us (92%)
  local copies, waits for them, and re-layouts  0.97 us (4%)
  between operations  0.66 us (3%)
    pallas_call x1, Pallas kernels, shards(): pl.pallas_call(functools.partial(kernel, sizes), out_shape=jax.ShapeDtype...  20.4 us
    unnamed x1, local copies, waits for them, and re-layouts  0.97 us

profile of v3, /device:TPU:0, one launch (start us, length us, event | category | flops | bytes accessed | tf_op | source)
XLA Modules:
  0.0 22.0 jit_solution(12247842279825212515)
XLA Ops:
  0.7 20.4 %shard_map.91 = bf16[256,2048]{1,0:T(8,128)(2,1)S(1)} custom-call(bf16[256,2048]{1,0:T(8,128)(2,1)} %dens_h.1, bf16[8192,128]{1,0:T(8,128)(2,1)} %bitcast.13, bf16[3,512,128]{2,1,0:T(8,128)(2,1)} %bitcast.15, bf16[3,512,128]{2,1,0:T(8,128)(2,1)} %bitcast.16, bf16[256,16,2,128]{3,2,1,0:T(2,128)(2,1)} %bitcast.14, bf16[64,256,128]{2,1,0:T(8,128)(2,1)} %bitcast.12, ...), custom_call_target="tpu_custom_call" | custom-call | tf_op jit(solution)/shard_map/pallas_call | solution.py:330
  21.1 1.0 %copy.13 = bf16[256,2048]{1,0:T(8,128)(2,1)} copy(bf16[256,2048]{1,0:T(8,128)(2,1)S(1)} %shard_map.91) | data formatting | bytes 2097152

commit v4 on v3

--- a/solution.py
+++ b/solution.py
@@ -76,8 +76,6 @@
         item.start()
     factors = (la_h, lb_h)
     loads_lev = [pltpu.make_async_copy(factors[ab], lev_v.at[ab, tgt], lev_sem.at[ab]) for ab in range(2)]
-    for item in loads_lev:
-        item.start()
     loads_tiles = [
         pltpu.make_async_copy(
             tiles_h.at[pl.ds(part * slots_part, slots_part)],
@@ -106,10 +104,6 @@
         for level in range(levels)
     ]
 
-    for item in loads_tiles:
-        item.start()
-    for item in loads_exp:
-        item.start()
     per_part = clusters // comp_parts
 
     def parts(buffer, stride, offset):
@@ -139,6 +133,12 @@
         for c in range(part * per_part, (part + 1) * per_part):
             split(c)
         total = total + squeeze(part, other)
+    for item in loads_tiles:
+        item.start()
+    for item in loads_exp:
+        item.start()
+    for item in loads_lev:
+        item.start()
     part_v[...] = total.astype(BF16)
     swap_part = pltpu.make_async_remote_copy(
         src_ref=part_v, dst_ref=part_r, send_sem=part_sem.at[0], recv_sem=part_sem.at[1],

time: 22.2 us -> 22.2 us (level)
  no operation moved by 1% of the time
where the time goes in v4:
time: 22.2 us; the launch traced here: 22 us
  Pallas kernels  20.4 us (92%)
  local copies, waits for them, and re-layouts  0.97 us (4%)
  between operations  0.66 us (3%)
    pallas_call x1, Pallas kernels, shards(): pl.pallas_call(functools.partial(kernel, sizes), out_shape=jax.ShapeDtype...  20.4 us
    unnamed x1, local copies, waits for them, and re-layouts  0.97 us

profile of v4, /device:TPU:0, one launch (start us, length us, event | category | flops | bytes accessed | tf_op | source)
XLA Modules:
  0.0 22.0 jit_solution(2167084971982043366)
XLA Ops:
  0.7 20.4 %shard_map.91 = bf16[256,2048]{1,0:T(8,128)(2,1)S(1)} custom-call(bf16[256,2048]{1,0:T(8,128)(2,1)} %dens_h.1, bf16[8192,128]{1,0:T(8,128)(2,1)} %bitcast.13, bf16[3,512,128]{2,1,0:T(8,128)(2,1)} %bitcast.15, bf16[3,512,128]{2,1,0:T(8,128)(2,1)} %bitcast.16, bf16[256,16,2,128]{3,2,1,0:T(2,128)(2,1)} %bitcast.14, bf16[64,256,128]{2,1,0:T(8,128)(2,1)} %bitcast.12, ...), custom_call_target="tpu_custom_call" | custom-call | tf_op jit(solution)/shard_map/pallas_call | solution.py:330
  21.1 1.0 %copy.13 = bf16[256,2048]{1,0:T(8,128)(2,1)} copy(bf16[256,2048]{1,0:T(8,128)(2,1)S(1)} %shard_map.91) | data formatting | bytes 2097152

commit v5 on v4

--- a/solution.py
+++ b/solution.py
@@ -176,7 +176,7 @@
     def send(level, q):
         copy = pltpu.make_async_remote_copy(
             src_ref=coef_v.at[level, q], dst_ref=recv_v.at[level, q],
-            send_sem=send_sem.at[level, q], recv_sem=recv_sem.at[level, q],
+            send_sem=send_sem, recv_sem=recv_sem.at[level, q],
             device_id=partners[level], device_id_type=MESH,
         )
         copy.start()
@@ -220,8 +220,6 @@
         point_v[c, :, width:] = dens_v[rhs:, cut]
     upper, lower = spread(width)
     current = sends
-    done_sends = []
-    swaps_fin = []
     for level in range(levels):
         prepare(level)
         own = matmul(
@@ -247,12 +245,10 @@
             else:
                 copy = pltpu.make_async_remote_copy(
                     src_ref=coef_v.at[levels, q], dst_ref=fin_r.at[q],
-                    send_sem=fin_sem.at[0, q], recv_sem=fin_sem.at[1, q],
+                    send_sem=fin_sem.at[0], recv_sem=fin_sem.at[1],
                     device_id=sibling, device_id_type=MESH,
                 )
                 copy.start()
-                swaps_fin.append(copy)
-        done_sends += current
         current = following
 
     origins = []
@@ -290,10 +286,9 @@
 
     all_turns.wait()
     finish(tgt, jnp.concatenate([coef_v[levels, q] for q in range(CHUNKS)], axis=0))
-    for item in done_sends:
-        item.wait_send()
-    for item in swaps_fin:
-        item.wait()
+    pltpu.make_async_copy(recv_v, recv_v, send_sem).wait()
+    for i in range(2):
+        pltpu.make_async_copy(fin_r, fin_r, fin_sem.at[i]).wait()
     finish(other, jnp.concatenate([fin_r[q] for q in range(CHUNKS)], axis=0))
 
 
@@ -360,9 +355,9 @@
             dma,
             dma((tile_parts,)),
             dma((2,)),
+            dma,
             dma((levels, CHUNKS)),
-            dma((levels, CHUNKS)),
-            dma((2, CHUNKS)),
+            dma((2,)),
             dma((2,)),
         ],
         compiler_params=pltpu.CompilerParams(

time: 22.2 us -> 22 us (level)
  no operation moved by 1% of the time
where the time goes in v5:
time: 22 us; the launch traced here: 21.9 us
  Pallas kernels  20.2 us (92%)
  local copies, waits for them, and re-layouts  0.97 us (4%)
  between operations  0.66 us (3%)
    pallas_call x1, Pallas kernels, shards(): pl.pallas_call(functools.partial(kernel, sizes), out_shape=jax.ShapeDtype...  20.2 us
    unnamed x1, local copies, waits for them, and re-layouts  0.97 us

profile of v5, /device:TPU:0, one launch (start us, length us, event | category | flops | bytes accessed | tf_op | source)
XLA Modules:
  0.0 21.9 jit_solution(6284455477098406219)
XLA Ops:
  0.7 20.2 %shard_map.91 = bf16[256,2048]{1,0:T(8,128)(2,1)S(1)} custom-call(bf16[256,2048]{1,0:T(8,128)(2,1)} %dens_h.1, bf16[8192,128]{1,0:T(8,128)(2,1)} %bitcast.13, bf16[3,512,128]{2,1,0:T(8,128)(2,1)} %bitcast.15, bf16[3,512,128]{2,1,0:T(8,128)(2,1)} %bitcast.16, bf16[256,16,2,128]{3,2,1,0:T(2,128)(2,1)} %bitcast.14, bf16[64,256,128]{2,1,0:T(8,128)(2,1)} %bitcast.12, ...), custom_call_target="tpu_custom_call" | custom-call | tf_op jit(solution)/shard_map/pallas_call | solution.py:325
  20.9 1.0 %copy.13 = bf16[256,2048]{1,0:T(8,128)(2,1)} copy(bf16[256,2048]{1,0:T(8,128)(2,1)S(1)} %shard_map.91) | data formatting | bytes 2097152
